TPU v7x, 128 devices: a whole 4x4x4 slice. The times are simulated.
128 devices in a mesh: dp: 32 (over x, y, core), group: 4 (over z).
Axes of the slice: x: 4, y: 4, z: 4, core: 2. Of those that a mesh axis runs over, the one named last changes fastest.
Arguments:
- images: bfloat16 [16384, 512], P(('dp', 'group')), may hold values from -1 to 1
- texts: bfloat16 [16384, 512], P(('dp', 'group')), may hold values from -1 to 1
- log_scale: float32 [], replicated, may hold values from 2 to 2.7
Outputs:
- grad_images: bfloat16 [16384, 512], P(('dp', 'group'))
- grad_texts: bfloat16 [16384, 512], P(('dp', 'group'))
- loss: float32 [], replicated
- grad_scale: float32 [], replicated
All inputs are finite; a program needn't handle non-finite values.
Results may differ from a plain program's by a relative error of at most 0.0013.
The roundings to bfloat16 on the way count: a program that leaves them out, or rounds other values in their place, can miss the bound.
Values may be sent and summed in bfloat16 or wider, within the bound.
No kernel may reach another device: no remote copies, remote signals or barrier semaphores. Data moves between devices by JAX's collectives and lax.ppermute only.
A program may use at most 128 MiB of HBM per device.

v0:
```python
import jax
import jax.numpy as jnp
from jax import lax
from jax.sharding import Mesh
from jax.sharding import PartitionSpec as P

DP_GROUP = ("dp_0", "dp_1", "dp_2", "group")


def in_one_piece(arrays, axis, split_dim, concat_dim, along):
    ends, at = ([], 0)
    for a in arrays[:-1]:
        at += a.shape[along]
        ends.append(at)
    both = jnp.concatenate(arrays, axis=along)
    return tuple(
        jnp.split(
            lax.all_to_all(both, axis, split_axis=split_dim, concat_axis=concat_dim, tiled=True),
            ends,
            axis=along,
        )
    )


def rows_first(arrays, axis, dims):
    turned = [jnp.moveaxis(a, dim, 0) for a, dim in zip(arrays, dims)]
    both = jnp.concatenate([t.reshape(len(t), -1) for t in turned], axis=1)
    filled, at, outs = (lax.all_gather(both, axis, axis=0, tiled=True), 0, [])
    for t, dim in zip(turned, dims):
        share = filled[:, at : at + t[0].size].reshape(-1, *t.shape[1:])
        outs.append(jnp.moveaxis(share, 0, dim))
        at += t[0].size
    return tuple(outs)


def one_axis_at_a_time(value, axes):
    for axis in axes:
        value = lax.psum(value, axis)
    return value


def body(images, texts, log_scale):
    row_count = images.shape[0]
    device_count = lax.axis_size(DP_GROUP)
    pair_total = row_count * device_count
    texts_whole = lax.all_gather(texts, DP_GROUP, axis=0, tiled=True)
    images_whole = lax.all_gather(images, DP_GROUP, axis=0, tiled=True)
    logit_scale = jnp.exp(log_scale)
    first_pair = lax.axis_index(DP_GROUP) * row_count
    contract_last = (((1,), (1,)), ((), ()))
    contract_first = (((0,), (0,)), ((), ()))
    row_logits = logit_scale * lax.dot_general(
        images, texts_whole, contract_last, preferred_element_type=jnp.float32
    )
    row_top = jnp.max(row_logits, axis=1)
    row_lse = row_top + jnp.log(jnp.sum(jnp.exp(row_logits - row_top[:, None]), axis=1))
    paired = jnp.diagonal(lax.dynamic_slice_in_dim(row_logits, first_pair, row_count, 1))
    part_top = jnp.max(row_logits, axis=0)
    part_sum = jnp.sum(jnp.exp(row_logits - part_top[None, :]), axis=0)
    got_top, got_sum = in_one_piece(
        (part_top.reshape(device_count, row_count), part_sum.reshape(device_count, row_count)),
        DP_GROUP,
        0,
        0,
        1,
    )
    col_top = jnp.max(got_top, axis=0)
    col_lse = col_top + jnp.log(jnp.sum(got_sum * jnp.exp(got_top - col_top[None, :]), axis=0))
    row_whole, col_whole = rows_first((row_lse, col_lse), DP_GROUP, (0, 0))
    own_pairs = (
        jnp.arange(pair_total)[None, :] == (first_pair + jnp.arange(row_count))[:, None]
    ).astype(jnp.float32)
    row_grad = (
        0.5 * (jnp.exp(row_logits - row_lse[:, None]) + jnp.exp(row_logits - col_whole[None, :]))
        - own_pairs
    )
    scale_part = jnp.sum(row_grad * row_logits)
    row_weights = row_grad.astype(jnp.bfloat16)
    grad_images = (
        logit_scale * jnp.dot(row_weights, texts_whole, preferred_element_type=jnp.float32)
    ).astype(jnp.bfloat16)
    col_logits = logit_scale * lax.dot_general(
        images_whole, texts, contract_last, preferred_element_type=jnp.float32
    )
    col_grad = (
        0.5 * (jnp.exp(col_logits - row_whole[:, None]) + jnp.exp(col_logits - col_lse[None, :]))
        - own_pairs.T
    )
    text_sum = logit_scale * lax.dot_general(
        col_grad.astype(jnp.bfloat16),
        images_whole,
        contract_first,
        preferred_element_type=jnp.float32,
    )
    grad_texts = text_sum.astype(jnp.bfloat16)
    loss_part = jnp.sum(row_lse) + jnp.sum(col_lse) - 2.0 * jnp.sum(paired)
    loss_total, scale_total = (
        one_axis_at_a_time(loss_part, DP_GROUP),
        one_axis_at_a_time(scale_part, DP_GROUP),
    )
    return (grad_images, grad_texts, loss_total / (2.0 * pair_total), scale_total / pair_total)


def solution(mesh):
    split = Mesh(
        mesh.devices.reshape(4, 4, 2, mesh.shape["group"]), ("dp_0", "dp_1", "dp_2", "group")
    )
    placed = (P(DP_GROUP, None), P(DP_GROUP, None), P())
    return jax.shard_map(
        body,
        mesh=split,
        in_specs=placed,
        out_specs=(P(DP_GROUP, None), P(DP_GROUP, None), P(), P()),
        check_vma=False,
    )
```

profile of v0, /device:TPU:0, one launch (start us, length us, event | category | flops | bytes accessed | tf_op | source)
XLA Modules:
  0.0 263.8 jit_solution(17786985613269034500)
XLA Ops:
  7.2 0.0 all-gather.3.cloned.1.call-start
  7.2 0.7 all-gather.3.cloned.1.call-update
  7.9 0.0 all-gather.5.cloned.1.call-start
  7.9 0.7 all-gather.5.cloned.1.call-update
  9.4 84.2 %all-gather.3.cloned.1.call-done = bf16[16384,512]{1,0:T(8,128)(2,1)} async-done(((bf16[128,512]{1,0:T(8,128)(2,1)}), bf16[16384,512]{1,0:T(8,128)(2,1)}) %all-gather.3.cloned.1.call-update) | async-done | bytes 16777232 | tf_op jit(solution)/shard_map/all_gather | solution.py:46
  93.6 14.5 %fusion.19 = (f32[128]{0:T(128)S(1)}, f32[16384]{0:T(1024)S(1)}, f32[128,16384]{1,0:T(8,128)}) fusion(bf16[128,512]{1,0:T(8,128)(2,1)} %param.3, bf16[16384,512]{1,0:T(8,128)(2,1)} %all-gather.3.cloned.1.call-done, f32[]{:T(128)S(6)} %exp.24), kind=kOutput, calls=%fused_computation.34 | convolution fusion | flops 2153758720 | bytes 25362948 | tf_op jit(solution)/shard_map/dot_general | solution.py:52
  108.1 4.7 %exponential_reduce_fusion.1 = (f32[128]{0:T(128)S(1)}, f32[16384]{0:T(1024)S(1)}) fusion(f32[128,16384]{1,0:T(8,128)} %get-tuple-element.22, f32[128]{0:T(128)S(1)} %get-tuple-element.6, f32[16384]{0:T(1024)S(1)} %get-tuple-element.7), kind=kLoop, calls=%fused_computation.9 | loop fusion | flops 8372096 | bytes 8520704 | tf_op jit(solution)/shard_map/reduce_sum | solution.py:56
  112.9 0.7 all_to_all.8
  113.6 8.2 %all-to-all-start = ((f32[128,1,256]{2,1,0:T(1,128)}), f32[128,1,256]{2,1,0:T(1,128)S(1)}, u32[]{:S(2)}, u32[]{:S(2)}) async-start(f32[128,1,256]{2,1,0:T(1,128)} %all_to_all.8), calls=%async_computation | async-start | bytes 262144 | tf_op jit(solution)/shard_map/all_to_all | solution.py:18
  121.9 0.9 constant_dynamic-slice_fusion
  122.7 1.2 gather_fusion
  124.0 0.6 reduce_sum.68
  125.2 0.6 fusion.21
  125.8 5.2 %all-to-all-done = f32[128,1,256]{2,1,0:T(1,128)S(1)} async-done(((f32[128,1,256]{2,1,0:T(1,128)}), f32[128,1,256]{2,1,0:T(1,128)S(1)}, u32[]{:S(2)}, u32[]{:S(2)}) %all-to-all-start) | async-done | bytes 131104 | tf_op jit(solution)/shard_map/all_to_all | solution.py:18
  131.1 0.6 fusion.20
  133.1 50.5 %all_gather.10 = f32[16384,2]{0,1:T(2,128)S(1)} all-gather(f32[128,2]{0,1:T(2,128)S(1)} %pad_maximum_fusion.1), channel_id=1, replica_groups=mesh['dp_0'=4,'dp_1'=4,'dp_2'=2,'group'=4] {'dp_0','dp_1','dp_2','group'}, dimensions={0}, use_global_device_ids=true | all-gather | bytes 132096 | tf_op jit(solution)/shard_map/all_gather | solution.py:28
  183.6 0.1 fusion.22
  183.7 6.5 %multiply_reduce_fusion = f32[]{:T(128)} fusion(f32[128,16384]{1,0:T(8,128)} %get-tuple-element.22, s32[128]{0:T(128)S(1)} %iota_add_fusion, f32[16384]{0:T(1024)S(1)} %bitcast.20, f32[128]{0:T(128)S(1)} %get-tuple-element.19), kind=kLoop, calls=%fused_computation.3 | loop fusion | flops 18874368 | bytes 8455172 | tf_op jit(solution)/shard_map/reduce_sum | solution.py:77
  190.2 10.4 %all-reduce.2 = (f32[]{:T(128)}, f32[]{:T(128)}) all-reduce(f32[]{:T(128)S(6)} %sub.87, f32[]{:T(128)} %multiply_reduce_fusion), channel_id=1, replica_groups=mesh['dp_0'=4,'dp_1'=4,'dp_2'=2,'group'=4] {'dp_0'}, use_global_device_ids=true, to_apply=%region_9.10 | all-reduce | flops 2 | bytes 16 | tf_op jit(solution)/shard_map/psum | solution.py:38
  200.6 8.8 %all-reduce.1 = (f32[]{:T(128)}, f32[]{:T(128)}) all-reduce(f32[]{:T(128)} %get-tuple-element.12, f32[]{:T(128)} %get-tuple-element.13), channel_id=1, replica_groups=mesh['dp_0'=4,'dp_1'=4,'dp_2'=2,'group'=4] {'dp_1'}, use_global_device_ids=true, to_apply=%region_10.11 | all-reduce | flops 2 | bytes 16 | tf_op jit(solution)/shard_map/psum | solution.py:38
  209.3 3.1 %all-reduce.3 = (f32[]{:T(128)}, f32[]{:T(128)}) all-reduce(f32[]{:T(128)} %get-tuple-element.10, f32[]{:T(128)} %get-tuple-element.11), channel_id=1, replica_groups=mesh['dp_0'=4,'dp_1'=4,'dp_2'=2,'group'=4] {'dp_2'}, use_global_device_ids=true, to_apply=%region_11.12 | all-reduce | flops 2 | bytes 16 | tf_op jit(solution)/shard_map/psum | solution.py:38
  212.4 10.0 %all-reduce = (f32[]{:T(128)}, f32[]{:T(128)}) all-reduce(f32[]{:T(128)} %get-tuple-element.14, f32[]{:T(128)} %get-tuple-element.15), channel_id=1, replica_groups=mesh['dp_0'=4,'dp_1'=4,'dp_2'=2,'group'=4] {'group'}, use_global_device_ids=true, to_apply=%region_12.13 | all-reduce | flops 2 | bytes 16 | tf_op jit(solution)/shard_map/psum | solution.py:38
  223.8 0.0 copy-start
  223.8 12.4 %fusion.12 = bf16[128,512]{1,0:T(8,128)(2,1)} fusion(bf16[16384,512]{1,0:T(8,128)(2,1)} %all-gather.3.cloned.1.call-done, f32[128,16384]{1,0:T(8,128)} %get-tuple-element.22, s32[128]{0:T(128)S(1)} %iota_add_fusion, f32[16384]{0:T(1024)S(1)} %bitcast.21, f32[128]{0:T(128)S(1)} %get-tuple-element.19, f32[]{:T(128)S(6)} %exp.24), kind=kOutput, calls=%fused_computation.19 | convolution fusion | flops 2164391936 | bytes 25363460 | tf_op jit(solution)/shard_map/dot_general | solution.py:80
  236.2 0.0 all-gather.5.cloned.1.call-done
  236.2 0.0 copy-done
  236.2 18.5 %fusion.15 = bf16[128,512]{1,0:T(8,128)(2,1)} fusion(bf16[16384,512]{1,0:T(8,128)(2,1)} %all-gather.5.cloned.1.call-done, bf16[128,512]{1,0:T(8,128)(2,1)S(1)} %copy-done, s32[128]{0:T(128)S(1)} %iota_add_fusion, f32[128]{0:T(128)S(1)} %get-tuple-element.17, f32[16384]{0:T(1024)S(1)} %bitcast.23, f32[]{:T(128)S(6)} %exp.24), kind=kOutput, calls=%fused_computation.20 | convolution fusion | flops 4313972736 | bytes 17105924 | tf_op jit(solution)/shard_map/dot_general | solution.py:89
  (7 shorter events, 0.1 us)
Async XLA Ops:
  7.2 86.4 %all-gather.3.cloned.1.call-start = ((), (), s32[]{:S(2)}) async-start(), calls=%async_computation.1 | async-start | bytes 16908288 | tf_op jit(solution)/shard_map/all_gather | solution.py:46
  7.9 228.3 %all-gather.5.cloned.1.call-start = ((), (), s32[]{:S(2)}) async-start(), calls=%async_computation.2 | async-start | bytes 16908288 | tf_op jit(solution)/shard_map/all_gather | solution.py:47
  113.6 17.4 %all-to-all-start = ((f32[128,1,256]{2,1,0:T(1,128)}), f32[128,1,256]{2,1,0:T(1,128)S(1)}, u32[]{:S(2)}, u32[]{:S(2)}) async-start(f32[128,1,256]{2,1,0:T(1,128)} %all_to_all.8), calls=%async_computation | async-start | bytes 262144 | tf_op jit(solution)/shard_map/all_to_all | solution.py:18
  223.8 12.4 %copy-start = (bf16[128,512]{1,0:T(8,128)(2,1)S(1)}, bf16[128,512]{1,0:T(8,128)(2,1)}, u32[]{:S(2)}) copy-start(bf16[128,512]{1,0:T(8,128)(2,1)} %param.4) | copy-start | bytes 393220
Sparse Core Ops, SparseCore 0:
  11.1 82.4 all-gather.2
  96.7 79.5 all-gather.4
where the time goes:
time: 264 us
  waiting for transfers between devices  90.8 us (34%)
  blocking collectives  82.8 us (31%)
  matrix products  45.4 us (17%)
  between operations  20.3 us (8%)
  other arithmetic  13.2 us (5%)
  starting transfers between devices  8.3 us (3%)
  local copies, waits for them, and re-layouts  2.96 us (1%)
    all_gather x1, waiting for transfers between devices, body(): texts_whole = lax.all_gather(texts, DP_GROUP, axis=0, tiled=True)  84.2 us
    all_gather x1, blocking collectives, rows_first(): filled, at, outs = (lax.all_gather(both, axis, axis=0, tiled=True), 0, [])  50.5 us
    psum x4, blocking collectives, one_axis_at_a_time(): value = lax.psum(value, axis)  32.3 us
    dot_general x1, matrix products, body(): lax.dot_general(col_grad.astype(jnp.bfloat16), images_whole, contract_fir...  18.5 us
    dot_general x1, matrix products, body(): lax.dot_general(images, texts_whole, contract_last, preferred_element_typ...  14.5 us
    dot_general x1, matrix products, body(): jnp.dot(row_weights, texts_whole, preferred_element_type=jnp.float32)  12.4 us
    all_to_all x1, starting transfers between devices, in_one_piece(): lax.all_to_all(both, axis, split_axis=split_dim, concat_axis=concat_dim,...  8.23 us
    reduce_sum x1, other arithmetic, body(): scale_part = jnp.sum(row_grad * row_logits)  6.49 us
  transfers between devices with their start and end apart: 3, of which 2 were waited for; matrix products, arithmetic and copies ran while one was open for 16% of the time, Pallas kernels for 0%

commit v1 on v0

--- a/solution.py
+++ b/solution.py
@@ -43,7 +43,10 @@
     row_count = images.shape[0]
     device_count = lax.axis_size(DP_GROUP)
     pair_total = row_count * device_count
-    texts_whole = lax.all_gather(texts, DP_GROUP, axis=0, tiled=True)
+    devices = lax.axis_size(DP_GROUP)
+    shards = jnp.stack([texts for _ in range(devices)])
+    shards = lax.all_to_all(shards, DP_GROUP, split_axis=0, concat_axis=0)
+    texts_whole = jnp.concatenate(shards, axis=0)
     images_whole = lax.all_gather(images, DP_GROUP, axis=0, tiled=True)
     logit_scale = jnp.exp(log_scale)
     first_pair = lax.axis_index(DP_GROUP) * row_count

time: 264 us -> 445 us (1.69)
  waiting for transfers between devices: 90.8 us -> 248 us
  starting transfers between devices: 8.3 us -> 27.4 us
  local copies, waits for them, and re-layouts: 2.96 us -> 9.67 us
    all_to_all x0 -> x1, waiting for transfers between devices: none -> 242 us  [body(): shards = lax.all_to_all(shards, DP_GROUP, split_axis=0, concat_axis=0)]
    all_gather x1 -> x0, waiting for transfers between devices: 84.2 us -> none  [body(): texts_whole = lax.all_gather(texts, DP_GROUP, axis=0, tiled=True)]
    all_to_all x0 -> x1, starting transfers between devices: none -> 11.7 us  [body(): shards = lax.all_to_all(shards, DP_GROUP, split_axis=0, concat_axis=0)]
    all_to_all x1, starting transfers between devices: 8.23 us -> 15.6 us  [in_one_piece(): lax.all_to_all(both, axis, split_axis=split_dim, concat_axis=concat_dim,...]
    another operation x0 -> x1, local copies, waits for them, and re-layouts: none -> 6.7 us  [body(): shards = jnp.stack([texts for _ in range(devices)])]
  transfers between devices with their start and end apart: 3 -> 3, of which waited for: 2 -> 2; matrix products, arithmetic and copies ran while one was open for 16% -> 11% of each run, Pallas kernels for 0% -> 0%
where the time goes in v1:
time: 445 us; the launch traced here: 444 us
  waiting for transfers between devices  248 us (56%)
  blocking collectives  80.1 us (18%)
  matrix products  45.5 us (10%)
  starting transfers between devices  27.4 us (6%)
  between operations  20.3 us (5%)
  other arithmetic  13.2 us (3%)
  local copies, waits for them, and re-layouts  9.67 us (2%)
    all_to_all x1, waiting for transfers between devices, body(): shards = lax.all_to_all(shards, DP_GROUP, split_axis=0, concat_axis=0)  242 us
    all_gather x1, blocking collectives, rows_first(): filled, at, outs = (lax.all_gather(both, axis, axis=0, tiled=True), 0, [])  47.8 us
    psum x4, blocking collectives, one_axis_at_a_time(): value = lax.psum(value, axis)  32.4 us
    dot_general x1, matrix products, body(): lax.dot_general(col_grad.astype(jnp.bfloat16), images_whole, contract_fir...  18.5 us
    all_to_all x1, starting transfers between devices, in_one_piece(): lax.all_to_all(both, axis, split_axis=split_dim, concat_axis=concat_dim,...  15.6 us
    dot_general x1, matrix products, body(): lax.dot_general(images, texts_whole, contract_last, preferred_element_typ...  14.6 us
    dot_general x1, matrix products, body(): jnp.dot(row_weights, texts_whole, preferred_element_type=jnp.float32)  12.4 us
    all_to_all x1, starting transfers between devices, body(): shards = lax.all_to_all(shards, DP_GROUP, split_axis=0, concat_axis=0)  11.7 us
  transfers between devices with their start and end apart: 3, of which 2 were waited for; matrix products, arithmetic and copies ran while one was open for 11% of the time, Pallas kernels for 0%

profile of v1, /device:TPU:0, one launch (start us, length us, event | category | flops | bytes accessed | tf_op | source)
XLA Modules:
  0.0 444.2 jit_solution(16378072612578555267)
XLA Ops:
  7.2 0.0 all-gather.2.cloned.1.call-start
  7.2 0.7 all-gather.2.cloned.1.call-update
  7.9 6.7 %stack.2 = bf16[128,128,512]{2,1,0:T(8,128)(2,1)} broadcast(bf16[128,512]{1,0:T(8,128)(2,1)} %param.4), dimensions={1,2} | broadcast | bytes 16908288 | tf_op jit(solution)/shard_map/stack | solution.py:47
  14.6 0.0 copy-start
  14.6 11.7 %all-to-all-start = ((bf16[128,128,512]{2,1,0:T(8,128)(2,1)}), bf16[128,128,512]{2,1,0:T(8,128)(2,1)}, u32[]{:S(2)}, u32[]{:S(2)}) async-start(bf16[128,128,512]{2,1,0:T(8,128)(2,1)} %stack.2), calls=%async_computation | async-start | bytes 33554432 | tf_op jit(solution)/shard_map/all_to_all | solution.py:48
  27.0 242.1 %all-to-all-done = bf16[128,128,512]{2,1,0:T(8,128)(2,1)} async-done(((bf16[128,128,512]{2,1,0:T(8,128)(2,1)}), bf16[128,128,512]{2,1,0:T(8,128)(2,1)}, u32[]{:S(2)}, u32[]{:S(2)}) %all-to-all-start) | async-done | bytes 16777248 | tf_op jit(solution)/shard_map/all_to_all | solution.py:48
  269.2 0.0 copy-done
  269.2 14.6 %fusion.19 = (f32[128]{0:T(128)S(1)}, f32[16384]{0:T(1024)S(1)}, f32[128,16384]{1,0:T(8,128)}) fusion(bf16[128,512]{1,0:T(8,128)(2,1)S(1)} %copy-done, bf16[16384,512]{1,0:T(8,128)(2,1)} %bitcast, f32[]{:T(128)S(6)} %exp.24), kind=kOutput, calls=%fused_computation.34 | convolution fusion | flops 2153758720 | bytes 25362948 | tf_op jit(solution)/shard_map/dot_general | solution.py:55
  283.8 4.7 %exponential_reduce_fusion.1 = (f32[128]{0:T(128)S(1)}, f32[16384]{0:T(1024)S(1)}) fusion(f32[128,16384]{1,0:T(8,128)} %get-tuple-element.22, f32[128]{0:T(128)S(1)} %get-tuple-element.6, f32[16384]{0:T(1024)S(1)} %get-tuple-element.7), kind=kLoop, calls=%fused_computation.9 | loop fusion | flops 8372096 | bytes 8520704 | tf_op jit(solution)/shard_map/reduce_sum | solution.py:59
  288.5 0.7 all_to_all.12
  289.3 15.6 %all-to-all-start.1 = ((f32[128,1,256]{2,1,0:T(1,128)}), f32[128,1,256]{2,1,0:T(1,128)S(1)}, u32[]{:S(2)}, u32[]{:S(2)}) async-start(f32[128,1,256]{2,1,0:T(1,128)} %all_to_all.12), calls=%async_computation.1 | async-start | bytes 262144 | tf_op jit(solution)/shard_map/all_to_all | solution.py:18
  304.9 0.9 constant_dynamic-slice_fusion
  305.8 1.2 gather_fusion
  307.0 0.6 reduce_sum.68
  308.3 0.6 fusion.21
  308.9 5.2 %all-to-all-done.1 = f32[128,1,256]{2,1,0:T(1,128)S(1)} async-done(((f32[128,1,256]{2,1,0:T(1,128)}), f32[128,1,256]{2,1,0:T(1,128)S(1)}, u32[]{:S(2)}, u32[]{:S(2)}) %all-to-all-start.1) | async-done | bytes 131104 | tf_op jit(solution)/shard_map/all_to_all | solution.py:18
  314.2 0.6 fusion.20
  316.1 47.8 %all_gather.6 = f32[16384,2]{0,1:T(2,128)S(1)} all-gather(f32[128,2]{0,1:T(2,128)S(1)} %pad_maximum_fusion.1), channel_id=1, replica_groups=mesh['dp_0'=4,'dp_1'=4,'dp_2'=2,'group'=4] {'dp_0','dp_1','dp_2','group'}, dimensions={0}, use_global_device_ids=true | all-gather | bytes 132096 | tf_op jit(solution)/shard_map/all_gather | solution.py:28
  363.9 0.1 fusion.22
  364.0 6.5 %multiply_reduce_fusion = f32[]{:T(128)} fusion(f32[128,16384]{1,0:T(8,128)} %get-tuple-element.22, s32[128]{0:T(128)S(1)} %iota_add_fusion, f32[16384]{0:T(1024)S(1)} %bitcast.21, f32[128]{0:T(128)S(1)} %get-tuple-element.19), kind=kLoop, calls=%fused_computation.3 | loop fusion | flops 18874368 | bytes 8455172 | tf_op jit(solution)/shard_map/reduce_sum | solution.py:80
  370.5 10.4 %all-reduce.2 = (f32[]{:T(128)}, f32[]{:T(128)}) all-reduce(f32[]{:T(128)S(6)} %sub.87, f32[]{:T(128)} %multiply_reduce_fusion), channel_id=1, replica_groups=mesh['dp_0'=4,'dp_1'=4,'dp_2'=2,'group'=4] {'dp_0'}, use_global_device_ids=true, to_apply=%region_9.10 | all-reduce | flops 2 | bytes 16 | tf_op jit(solution)/shard_map/psum | solution.py:38
  380.9 8.8 %all-reduce.1 = (f32[]{:T(128)}, f32[]{:T(128)}) all-reduce(f32[]{:T(128)} %get-tuple-element.12, f32[]{:T(128)} %get-tuple-element.13), channel_id=1, replica_groups=mesh['dp_0'=4,'dp_1'=4,'dp_2'=2,'group'=4] {'dp_1'}, use_global_device_ids=true, to_apply=%region_10.11 | all-reduce | flops 2 | bytes 16 | tf_op jit(solution)/shard_map/psum | solution.py:38
  389.7 3.1 all-reduce.3
  392.8 10.1 %all-reduce = (f32[]{:T(128)}, f32[]{:T(128)}) all-reduce(f32[]{:T(128)} %get-tuple-element.14, f32[]{:T(128)} %get-tuple-element.15), channel_id=1, replica_groups=mesh['dp_0'=4,'dp_1'=4,'dp_2'=2,'group'=4] {'group'}, use_global_device_ids=true, to_apply=%region_12.13 | all-reduce | flops 2 | bytes 16 | tf_op jit(solution)/shard_map/psum | solution.py:38
  404.2 0.0 copy-start.1
  404.2 12.4 %fusion.12 = bf16[128,512]{1,0:T(8,128)(2,1)} fusion(bf16[16384,512]{1,0:T(8,128)(2,1)} %bitcast, f32[128,16384]{1,0:T(8,128)} %get-tuple-element.22, s32[128]{0:T(128)S(1)} %iota_add_fusion, f32[16384]{0:T(1024)S(1)} %bitcast.22, f32[128]{0:T(128)S(1)} %get-tuple-element.19, f32[]{:T(128)S(6)} %exp.24), kind=kOutput, calls=%fused_computation.19 | convolution fusion | flops 2164391936 | bytes 25363460 | tf_op jit(solution)/shard_map/dot_general | solution.py:83
  416.6 0.0 all-gather.2.cloned.1.call-done
  416.6 0.0 copy-done.1
  416.6 18.5 %fusion.15 = bf16[128,512]{1,0:T(8,128)(2,1)} fusion(bf16[16384,512]{1,0:T(8,128)(2,1)} %all-gather.2.cloned.1.call-done, bf16[128,512]{1,0:T(8,128)(2,1)S(1)} %copy-done.1, s32[128]{0:T(128)S(1)} %iota_add_fusion, f32[128]{0:T(128)S(1)} %get-tuple-element.17, f32[16384]{0:T(1024)S(1)} %bitcast.24, f32[]{:T(128)S(6)} %exp.24), kind=kOutput, calls=%fused_computation.20 | convolution fusion | flops 4313972736 | bytes 17105924 | tf_op jit(solution)/shard_map/dot_general | solution.py:92
  (7 shorter events, 0.1 us)
Async XLA Ops:
  7.2 409.4 %all-gather.2.cloned.1.call-start = ((), (), s32[]{:S(2)}) async-start(), calls=%async_computation.2 | async-start | bytes 16908288 | tf_op jit(solution)/shard_map/all_gather | solution.py:50
  14.6 254.6 %copy-start = (bf16[128,512]{1,0:T(8,128)(2,1)S(1)}, bf16[128,512]{1,0:T(8,128)(2,1)}, u32[]{:S(2)}) copy-start(bf16[128,512]{1,0:T(8,128)(2,1)} %param.3) | copy-start | bytes 393220
  14.6 254.6 %all-to-all-start = ((bf16[128,128,512]{2,1,0:T(8,128)(2,1)}), bf16[128,128,512]{2,1,0:T(8,128)(2,1)}, u32[]{:S(2)}, u32[]{:S(2)}) async-start(bf16[128,128,512]{2,1,0:T(8,128)(2,1)} %stack.2), calls=%async_computation | async-start | bytes 33554432 | tf_op jit(solution)/shard_map/all_to_all | solution.py:48
  289.3 24.9 %all-to-all-start.1 = ((f32[128,1,256]{2,1,0:T(1,128)}), f32[128,1,256]{2,1,0:T(1,128)S(1)}, u32[]{:S(2)}, u32[]{:S(2)}) async-start(f32[128,1,256]{2,1,0:T(1,128)} %all_to_all.12), calls=%async_computation.1 | async-start | bytes 262144 | tf_op jit(solution)/shard_map/all_to_all | solution.py:18
  404.2 12.4 %copy-start.1 = (bf16[128,512]{1,0:T(8,128)(2,1)S(1)}, bf16[128,512]{1,0:T(8,128)(2,1)}, u32[]{:S(2)}) copy-start(bf16[128,512]{1,0:T(8,128)(2,1)} %param.4) | copy-start | bytes 393220
Sparse Core Ops, SparseCore 0:
  11.1 257.7 all-gather.1
